TPU v7x, 256 devices: a whole 4x4x8 slice. The times are simulated.
256 devices in a mesh: pb: 16 (over y_hi, x, core), wa: 16 (over y_lo, z).
Axes of the slice: x: 4, y: 4 (y_hi: 2, y_lo: 2; y = y_hi * 2 + y_lo), z: 8, core: 2. Of those that a mesh axis runs over, the one named last changes fastest.
Arguments:
- acts: bfloat16 [4096, 28672], P('pb', 'wa'), may hold values from -6 to 6
- grads: bfloat16 [4096, 8192], P('pb', 'wa'), may hold values from -6 to 6
- query_in: bfloat16 [28672, 4096], P('wa', 'pb'), may hold values from -0.03125 to 0.03125
- query_out: bfloat16 [8192, 4096], P('wa', 'pb'), may hold values from -0.01171875 to 0.01171875
- lengths: int32 [256], replicated, may hold values from 1 to 128, 4096 in all
Outputs:
- seq_scores: float32 [128, 256], P('pb', 'wa')
Inputs may be any that keep to these rules, and one draw needn't show every extreme that they name: The lengths sum to 4096 and the longest is exactly 128.
All inputs are finite; a program needn't handle non-finite values.
Results may differ from a plain program's by a relative error of at most 0.0003.
Values may be sent and summed in bfloat16 or wider, within the bound.
No kernel may reach another device: no remote copies, remote signals or barrier semaphores. Data moves between devices by JAX's collectives and lax.ppermute only.
A program may use at most 64 MiB of HBM per device.

v0:
```python
import functools

import jax
import jax.numpy as jnp
from jax import lax
from jax.experimental import pallas as pl
from jax.experimental.pallas import tpu as pltpu
from jax.sharding import PartitionSpec as P


RANK = 32
LANES = 128
LARGEST = 32000.0
WIDTH = 256


def moved(value, pairs):
    return lax.ppermute(value, "pb", pairs)


def code(part, slot, out_ref):
    width, rows, tags = part.shape[1], out_ref.shape[0], out_ref.shape[1] - LANES
    lane = lax.broadcasted_iota(jnp.int32, (rows, LANES), 1)
    largest = jnp.maximum(jnp.max(jnp.abs(part), axis=1, keepdims=True), 1e-25)
    power = jnp.floor(jnp.log2(LARGEST / largest))
    coded = jnp.round(part * jnp.exp2(power)).astype(jnp.int32)
    out_ref[:, slot * width : (slot + 1) * width] = coded.astype(jnp.int16)
    held = out_ref[:, tags:].astype(jnp.int32)
    tag = jnp.where(lane == slot, power.astype(jnp.int32), held)
    out_ref[:, tags:] = tag.astype(jnp.int16)


def put(slot, tokens, queries, out_ref):
    part = jnp.dot(tokens[...], queries[...], preferred_element_type=jnp.float32)
    code(part, slot, out_ref)


def near_rows(even_ref, own, side, flip, last, lasts, queries, out_ref):
    out_ref[:, out_ref.shape[1] - LANES :] = jnp.zeros((out_ref.shape[0], LANES), jnp.int16)
    put(0, own, queries, out_ref)

    @pl.when(even_ref[0] == 1)
    def _():
        put(1, flip, queries, out_ref)

    @pl.when(even_ref[0] == 0)
    def _():
        put(1, side, queries, out_ref)

    put(2, last, queries, out_ref)
    put(3, lasts, queries, out_ref)


def far_rows(own, side, last, lasts, queries, out_ref):
    put(4, own, queries, out_ref)
    put(5, side, queries, out_ref)
    put(6, last, queries, out_ref)
    put(7, lasts, queries, out_ref)


def rest_kernel(even, own, side, flip, last, lasts, near, far, out_ref):
    near_rows(even, own, side, flip, last, lasts, near, out_ref)
    far_rows(own, side, last, lasts, far, out_ref)


def near_kernel(even, own, side, flip, last, lasts, near, out_ref):
    near_rows(even, own, side, flip, last, lasts, near, out_ref)


def far_kernel(even, own, side, last, lasts, far, begun, out_ref):
    lanes = begun.shape[1] - LANES
    out_ref[:, :lanes] = begun[:, :lanes]
    out_ref[:, out_ref.shape[1] - LANES :] = begun[:, lanes:]
    far_rows(own, side, last, lasts, far, out_ref)


def decoded(came_ref, rows):
    lanes = came_ref.shape[1] - LANES
    undo = jnp.exp2(-came_ref[:, lanes:].astype(jnp.int32).astype(jnp.float32))
    pieces = []
    for slot in range(lanes // WIDTH):
        total = jnp.zeros((rows, WIDTH), jnp.float32)
        for at in range(0, came_ref.shape[0], rows):
            values = came_ref[at : at + rows, slot * WIDTH : (slot + 1) * WIDTH]
            scale = undo[at : at + rows, slot : slot + 1]
            total = total + values.astype(jnp.int32).astype(jnp.float32) * scale
        pieces.append(total)
    return pieces


def open_kernel(rows, came_ref, out_ref):
    for slot, piece in enumerate(decoded(came_ref, rows)):
        out_ref[slot * rows : (slot + 1) * rows, :] = piece


def close_kernel(rows, came_ref, outs_ref, near_ref, far_ref, out_ref):
    products = [
        piece * outs_ref[slot * rows : (slot + 1) * rows, :]
        for slot, piece in enumerate(decoded(came_ref, rows))
    ]
    half, queries = len(products) // 2, WIDTH // RANK
    for at, (group, table) in enumerate(
        [(products[:half], near_ref), (products[half:], far_ref)]
    ):
        by_rank = lax.dot_general(
            jnp.concatenate(group, axis=0),
            table[...],
            (((0,), (0,)), ((), ())),
            precision=lax.Precision.HIGHEST,
            preferred_element_type=jnp.float32,
        )
        total = jnp.sum(by_rank.reshape(queries, RANK, by_rank.shape[1]), axis=1)
        out_ref[at * queries : (at + 1) * queries, :] = total


def small(kernel, shape, arrays):
    return pl.pallas_call(
        kernel,
        out_shape=jax.ShapeDtypeStruct(shape, jnp.float32),
        compiler_params=pltpu.CompilerParams(vmem_limit_bytes=16 << 20),
        cost_estimate=pl.CostEstimate(
            flops=4 * arrays[0].size, bytes_accessed=2 * arrays[0].size, transcendentals=0
        ),
    )(*arrays)


def call(kernel, slots, scalar, arrays, scratch=()):
    rows, depth = arrays[0].shape
    lanes = slots * WIDTH
    vmem = pl.BlockSpec(memory_space=pltpu.VMEM)
    return pl.pallas_call(
        kernel,
        out_shape=jax.ShapeDtypeStruct((rows, lanes + LANES), jnp.int16),
        in_specs=[pl.BlockSpec(memory_space=pltpu.SMEM)] + [vmem] * len(arrays),
        out_specs=vmem,
        scratch_shapes=list(scratch),
        compiler_params=pltpu.CompilerParams(vmem_limit_bytes=16 << 20),
        cost_estimate=pl.CostEstimate(
            flops=2 * rows * depth * lanes,
            bytes_accessed=sum(a.size for a in arrays) * 2 + 2 * rows * lanes,
            transcendentals=0,
        ),
    )(scalar, *arrays)


def exchanged(coded):
    return lax.all_to_all(coded, "wa", 0, 0, tiled=True)


def member_table(starts, ends, first, count):
    spots = first + lax.iota(jnp.int32, count)
    inside = (spots[:, None] >= starts[None, :]) & (spots[:, None] < ends[None, :])
    return inside.astype(jnp.float32)


def scores(acts, grads, query_in, query_out, lengths):
    groups = lax.axis_size("pb")
    widths = lax.axis_size("wa")
    group = lax.axis_index("pb")
    width_slot = lax.axis_index("wa")
    quarter, half = groups // 4, groups // 2
    tok = acts.shape[0]
    rows = tok // widths
    nseq = lengths.shape[0]
    even = group % 2 == 0

    swap = [(p, p ^ 1) for p in range(groups)]
    ahead = [(p, (p + 2) % groups) for p in range(groups)]
    back = [(p, (p - quarter) % groups) for p in range(groups)]
    flip = [(p, (p - 1 + half) % groups) for p in range(1, groups, 2)]

    side_out = moved(grads, swap)
    last_out = moved(grads, ahead)
    far_out = moved(query_out, back)
    flip_out = moved(grads, flip)
    last_in = moved(acts, ahead)
    far_in = moved(query_in, back)
    flip_in = moved(acts, flip)
    side_in = moved(acts, swap)
    lasts_out = moved(last_out, swap)
    lasts_in = moved(last_in, swap)
    parity = even.astype(jnp.int32).reshape(1)
    coded_out = call(
        rest_kernel, 8, parity, [grads, side_out, flip_out, last_out, lasts_out, query_out, far_out]
    )
    came_out = exchanged(coded_out)
    outs = small(functools.partial(open_kernel, rows), (8 * rows, WIDTH), [came_out])
    near_in = call(near_kernel, 4, parity, [acts, side_in, flip_in, last_in, lasts_in, query_in])
    coded_in = call(far_kernel, 8, parity, [acts, side_in, last_in, lasts_in, far_in, near_in])
    came_in = exchanged(coded_in)
    ends = jnp.cumsum(lengths)
    starts = ends - lengths

    def table(block):
        return member_table(starts, ends, block * tok + width_slot * rows, rows)

    here, side = group, group ^ 1
    edge = jnp.where(even, (group + groups - half + 1) % groups, side)
    last, lasts = (group + groups - 2) % groups, (side + groups - 2) % groups
    t_own, t_side, t_edge, t_last, t_lasts = [table(b) for b in (here, side, edge, last, lasts)]

    near_table = jnp.concatenate([t_own, t_edge, t_last, t_lasts], axis=0)
    far_table = jnp.concatenate([t_own, t_side, t_last, t_lasts], axis=0)
    queries = query_in.shape[1] // RANK
    both = small(
        functools.partial(close_kernel, rows),
        (2 * queries, nseq),
        [came_in, outs, near_table, far_table],
    )
    share = nseq // widths
    both = jnp.moveaxis(both.reshape(both.shape[0], widths, share), 1, 0)
    came = jnp.sum(lax.all_to_all(both, "wa", 0, 0, tiled=True), axis=0)
    forward = [(p, (p + quarter) % groups) for p in range(groups)]
    mine = came[:queries] + moved(came[queries:], forward)
    lengths_float = lengths.astype(jnp.float32)
    my_lengths = lax.dynamic_slice_in_dim(lengths_float, width_slot * share, share, 0)
    return mine / my_lengths[None, :]


def solution(mesh):
    return jax.shard_map(
        scores,
        mesh=mesh,
        in_specs=(P("pb", "wa"), P("pb", "wa"), P("wa", "pb"), P("wa", "pb"), P()),
        out_specs=P("pb", "wa"),
        check_vma=False,
    )
```

profile of v0, /device:TPU:6, one launch (start us, length us, event | category | flops | bytes accessed | tf_op | source)
XLA Modules:
  0.0 159.7 jit_solution(9356316739615113484)
XLA Ops:
  0.0 3.1 %collective-permute-start.7 = (bf16[256,512]{1,0:T(8,128)(2,1)}, bf16[256,512]{1,0:T(8,128)(2,1)S(1)}, u32[]{:S(2)}, u32[]{:S(2)}) collective-permute-start(bf16[256,512]{1,0:T(8,128)(2,1)} %own.5), channel_id=1, source_target_pairs={{0,32},{16,48},{32,64},{48,80},{64,96},{80,112},{96,128},{112,144}... | collective-permute-start | bytes 786440 | tf_op jit(solution)/shard_map/ppermute | solution.py:18
  3.1 1.3 collective-permute-start.6
  4.4 0.1 collective-permute-start.9
  4.5 10.1 %collective-permute-done.7.last = bf16[256,512]{1,0:T(8,128)(2,1)S(1)} collective-permute-done((bf16[256,512]{1,0:T(8,128)(2,1)}, bf16[256,512]{1,0:T(8,128)(2,1)S(1)}, u32[]{:S(2)}, u32[]{:S(2)}) %collective-permute-start.7) | collective-permute-done | bytes 262176 | tf_op jit(solution)/shard_map/ppermute | solution.py:18
  14.6 6.0 %collective-permute-start.1 = (bf16[256,1792]{1,0:T(8,128)(2,1)}, bf16[256,1792]{1,0:T(8,128)(2,1)}, u32[]{:S(2)}, u32[]{:S(2)}) collective-permute-start(bf16[256,1792]{1,0:T(8,128)(2,1)} %own.4), channel_id=1, source_target_pairs={{0,32},{16,48},{32,64},{48,80},{64,96},{80,112},{96,128},{112,144}... | collective-permute-start | bytes 2752520 | tf_op jit(solution)/shard_map/ppermute | solution.py:18
  20.6 0.9 copy-done.2
  21.6 0.9 copy-done.3
  22.5 2.5 %shard_map.57 = s16[256,2176]{1,0:T(8,128)(2,1)} custom-call(s32[1]{0:T(128)} %bitcast.even, bf16[256,512]{1,0:T(8,128)(2,1)S(1)} %copy-done.2, bf16[256,512]{1,0:T(8,128)(2,1)S(1)} %collective-permute-done.5.side, bf16[256,512]{1,0:T(8,128)(2,1)S(1)} %collective-permute-done.6.flip, bf16[256,512]{1,0:T(8,128)(2,1)S(1)} %collective-permute-done.7.last, ...), custom_call_target="tpu_custom_call" | custom-call | flops 536870912 | bytes 2883584 | tf_op jit(solution)/shard_map/pallas_call | solution.py:131
  25.0 8.8 %all-to-all-start.1 = ((s16[16,16,2176]{2,1,0:T(8,128)(2,1)}), s16[16,16,2176]{2,1,0:T(8,128)(2,1)S(1)}, u32[]{:S(2)}, u32[]{:S(2)}) async-start(s16[16,16,2176]{2,1,0:T(8,128)(2,1)} %bitcast.3), calls=%async_computation.1 | async-start | bytes 2228224 | tf_op jit(solution)/shard_map/all_to_all | solution.py:147
  33.9 0.1 collective-permute-start
  34.0 1.3 collective-permute-start.4
  35.3 29.0 %collective-permute-done.1.last = bf16[256,1792]{1,0:T(8,128)(2,1)} collective-permute-done((bf16[256,1792]{1,0:T(8,128)(2,1)}, bf16[256,1792]{1,0:T(8,128)(2,1)}, u32[]{:S(2)}, u32[]{:S(2)}) %collective-permute-start.1) | collective-permute-done | bytes 917536 | tf_op jit(solution)/shard_map/ppermute | solution.py:18
  64.4 2.7 %collective-permute-done.2.lasts = bf16[256,1792]{1,0:T(8,128)(2,1)S(1)} collective-permute-done((bf16[256,1792]{1,0:T(8,128)(2,1)}, bf16[256,1792]{1,0:T(8,128)(2,1)S(1)}, u32[]{:S(2)}, u32[]{:S(2)}) %collective-permute-start.2) | collective-permute-done | bytes 917536 | tf_op jit(solution)/shard_map/ppermute | solution.py:18
  67.0 3.0 %shard_map.55.begun = s16[256,1152]{1,0:T(8,128)(2,1)S(1)} custom-call(s32[1]{0:T(128)} %bitcast.even, bf16[256,1792]{1,0:T(8,128)(2,1)S(1)} %copy-done.1, bf16[256,1792]{1,0:T(8,128)(2,1)S(1)} %collective-permute-done.side, bf16[256,1792]{1,0:T(8,128)(2,1)S(1)} %collective-permute-done.4.flip, bf16[256,1792]{1,0:T(8,128)(2,1)} %collective-permute-done.1.last, ...), custom_call_target="tpu_custom_call" | custom-call | flops 939524096 | bytes 6029312 | tf_op jit(solution)/shard_map/pallas_call | solution.py:131
  70.0 23.1 %collective-permute-done.3.far = bf16[1792,256]{1,0:T(8,128)(2,1)S(1)} collective-permute-done((bf16[1792,256]{1,0:T(8,128)(2,1)S(1)}, bf16[1792,256]{1,0:T(8,128)(2,1)S(1)}, u32[]{:S(2)}, u32[]{:S(2)}) %collective-permute-start.3) | collective-permute-done | bytes 917536 | tf_op jit(solution)/shard_map/ppermute | solution.py:18
  93.1 3.5 %shard_map.56 = s16[256,2176]{1,0:T(8,128)(2,1)} custom-call(s32[1]{0:T(128)} %bitcast.even, bf16[256,1792]{1,0:T(8,128)(2,1)S(1)} %copy-done.1, bf16[256,1792]{1,0:T(8,128)(2,1)S(1)} %collective-permute-done.side, bf16[256,1792]{1,0:T(8,128)(2,1)} %collective-permute-done.1.last, bf16[256,1792]{1,0:T(8,128)(2,1)S(1)} %collective-permute-done.2.lasts, ...), custom_call_target="tpu_custom_call" | custom-call | flops 1879048192 | bytes 6225920 | tf_op jit(solution)/shard_map/pallas_call | solution.py:131
  96.6 13.5 %all-to-all-start = ((s16[16,16,2176]{2,1,0:T(8,128)(2,1)}), s16[16,16,2176]{2,1,0:T(8,128)(2,1)S(1)}, u32[]{:S(2)}, u32[]{:S(2)}) async-start(s16[16,16,2176]{2,1,0:T(8,128)(2,1)} %bitcast.1), calls=%async_computation | async-start | bytes 2228224 | tf_op jit(solution)/shard_map/all_to_all | solution.py:147
  110.2 0.3 reduce-window.9
  110.6 0.1 slice_reduce_fusion
  110.8 0.1 and_convert_fusion
  110.9 0.4 shard_map.58.outs_ref
  111.3 25.9 %all-to-all-done = s16[16,16,2176]{2,1,0:T(8,128)(2,1)S(1)} async-done(((s16[16,16,2176]{2,1,0:T(8,128)(2,1)}), s16[16,16,2176]{2,1,0:T(8,128)(2,1)S(1)}, u32[]{:S(2)}, u32[]{:S(2)}) %all-to-all-start) | async-done | bytes 1114144 | tf_op jit(solution)/shard_map/all_to_all | solution.py:147
  137.2 1.7 %shard_map.59 = f32[16,256]{1,0:T(8,128)S(1)} custom-call(s16[256,2176]{1,0:T(8,128)(2,1)S(1)} %bitcast.13, f32[128,256]{1,0:T(8,128)S(1)} %shard_map.58.outs_ref, f32[64,256]{1,0:T(8,128)S(1)} %get-tuple-element.8.near_ref, f32[64,256]{1,0:T(8,128)S(1)} %get-tuple-element.7.far_ref), custom_call_target="tpu_custom_call" | custom-call | flops 2228224 | bytes 1114112 | tf_op jit(solution)/shard_map/pallas_call | solution.py:117
  138.9 0.1 reshape.64
  139.0 0.1 reshape.68
  139.1 13.4 %all_to_all.27 = f32[16,1,256]{2,1,0:T(1,128)S(1)} all-to-all(f32[16,1,256]{2,1,0:T(1,128)S(1)} %reshape.68), channel_id=1, replica_groups=mesh['pb'=16,'wa'=16] {'wa'}, dimensions={0} | all-to-all | bytes 32768 | tf_op jit(solution)/shard_map/all_to_all | solution.py:212
  152.6 0.5 broadcast.36
  153.1 0.7 reduce.2
  153.8 0.1 reshape.69
  153.9 0.1 collective-permute-start.10
  154.1 5.0 %collective-permute-done.10 = f32[8,16]{1,0:T(8,128)S(1)} collective-permute-done((f32[8,16]{1,0:T(8,128)S(1)}, f32[8,16]{1,0:T(8,128)S(1)}, u32[]{:S(2)}, u32[]{:S(2)}) %collective-permute-start.10) | collective-permute-done | bytes 544 | tf_op jit(solution)/shard_map/ppermute | solution.py:18
  159.1 0.6 fusion
  (30 shorter events, 0.4 us)
Async XLA Ops:
  0.0 14.6 %collective-permute-start.7 = (bf16[256,512]{1,0:T(8,128)(2,1)}, bf16[256,512]{1,0:T(8,128)(2,1)S(1)}, u32[]{:S(2)}, u32[]{:S(2)}) collective-permute-start(bf16[256,512]{1,0:T(8,128)(2,1)} %own.5), channel_id=1, source_target_pairs={{0,32},{16,48},{32,64},{48,80},{64,96},{80,112},{96,128},{112,144}... | collective-permute-start | bytes 786440 | tf_op jit(solution)/shard_map/ppermute | solution.py:18
  3.1 17.5 %collective-permute-start.5 = (bf16[256,512]{1,0:T(8,128)(2,1)}, bf16[256,512]{1,0:T(8,128)(2,1)S(1)}, u32[]{:S(2)}, u32[]{:S(2)}) collective-permute-start(bf16[256,512]{1,0:T(8,128)(2,1)} %own.5), channel_id=1, source_target_pairs={{0,16},{16,0},{32,48},{48,32},{64,80},{80,64},{96,112},{112,96},{1... | collective-permute-start | bytes 786440 | tf_op jit(solution)/shard_map/ppermute | solution.py:18
  3.1 17.5 %collective-permute-start.6 = (bf16[256,512]{1,0:T(8,128)(2,1)}, bf16[256,512]{1,0:T(8,128)(2,1)S(1)}, u32[]{:S(2)}, u32[]{:S(2)}) collective-permute-start(bf16[256,512]{1,0:T(8,128)(2,1)} %own.5), channel_id=1, source_target_pairs={{16,128},{48,160},{80,192},{112,224},{144,0},{176,32},{208,64},{24... | collective-permute-start | bytes 786440 | tf_op jit(solution)/shard_map/ppermute | solution.py:18
  4.4 16.2 %collective-permute-start.9 = (bf16[512,256]{1,0:T(8,128)(2,1)}, bf16[512,256]{1,0:T(8,128)(2,1)S(1)}, u32[]{:S(2)}, u32[]{:S(2)}) collective-permute-start(bf16[512,256]{1,0:T(8,128)(2,1)} %near.3), channel_id=1, source_target_pairs={{0,192},{16,208},{32,224},{48,240},{64,0},{80,16},{96,32},{112,48}... | collective-permute-start | bytes 786440 | tf_op jit(solution)/shard_map/ppermute | solution.py:18
  14.6 6.0 %collective-permute-start.8 = (bf16[256,512]{1,0:T(8,128)(2,1)S(1)}, bf16[256,512]{1,0:T(8,128)(2,1)S(1)}, u32[]{:S(2)}, u32[]{:S(2)}) collective-permute-start(bf16[256,512]{1,0:T(8,128)(2,1)S(1)} %collective-permute-done.7.last), channel_id=1, source_target_pairs={{0,16},{16,0},{32,48},{48,32},{64,80},{80,64},{96,112},{112,96},{1... | collective-permute-start | bytes 786440 | tf_op jit(solution)/shard_map/ppermute | solution.py:18
  14.6 49.7 %collective-permute-start.1 = (bf16[256,1792]{1,0:T(8,128)(2,1)}, bf16[256,1792]{1,0:T(8,128)(2,1)}, u32[]{:S(2)}, u32[]{:S(2)}) collective-permute-start(bf16[256,1792]{1,0:T(8,128)(2,1)} %own.4), channel_id=1, source_target_pairs={{0,32},{16,48},{32,64},{48,80},{64,96},{80,112},{96,128},{112,144}... | collective-permute-start | bytes 2752520 | tf_op jit(solution)/shard_map/ppermute | solution.py:18
  20.6 1.0 copy-start.2
  21.6 0.9 copy-start.3
  25.0 8.8 %copy-start.1 = (bf16[256,1792]{1,0:T(8,128)(2,1)S(1)}, bf16[256,1792]{1,0:T(8,128)(2,1)}, u32[]{:S(2)}) copy-start(bf16[256,1792]{1,0:T(8,128)(2,1)} %own.4) | copy-start | bytes 2752516
  25.0 39.3 %copy-start = (bf16[1792,256]{1,0:T(8,128)(2,1)S(1)}, bf16[1792,256]{1,0:T(8,128)(2,1)}, u32[]{:S(2)}) copy-start(bf16[1792,256]{1,0:T(8,128)(2,1)} %near.2) | copy-start | bytes 2752516
  25.0 71.6 %all-to-all-start.1 = ((s16[16,16,2176]{2,1,0:T(8,128)(2,1)}), s16[16,16,2176]{2,1,0:T(8,128)(2,1)S(1)}, u32[]{:S(2)}, u32[]{:S(2)}) async-start(s16[16,16,2176]{2,1,0:T(8,128)(2,1)} %bitcast.3), calls=%async_computation.1 | async-start | bytes 2228224 | tf_op jit(solution)/shard_map/all_to_all | solution.py:147
  33.9 30.5 %collective-permute-start = (bf16[256,1792]{1,0:T(8,128)(2,1)S(1)}, bf16[256,1792]{1,0:T(8,128)(2,1)S(1)}, u32[]{:S(2)}, u32[]{:S(2)}) collective-permute-start(bf16[256,1792]{1,0:T(8,128)(2,1)S(1)} %copy-done.1), channel_id=1, source_target_pairs={{0,16},{16,0},{32,48},{48,32},{64,80},{80,64},{96,112},{112,96},{1... | collective-permute-start | bytes 2752520 | tf_op jit(solution)/shard_map/ppermute | solution.py:18
  34.0 30.4 %collective-permute-start.4 = (bf16[256,1792]{1,0:T(8,128)(2,1)S(1)}, bf16[256,1792]{1,0:T(8,128)(2,1)S(1)}, u32[]{:S(2)}, u32[]{:S(2)}) collective-permute-start(bf16[256,1792]{1,0:T(8,128)(2,1)S(1)} %copy-done.1), channel_id=1, source_target_pairs={{16,128},{48,160},{80,192},{112,224},{144,0},{176,32},{208,64},{24... | collective-permute-start | bytes 2752520 | tf_op jit(solution)/shard_map/ppermute | solution.py:18
  64.3 2.7 %collective-permute-start.2 = (bf16[256,1792]{1,0:T(8,128)(2,1)}, bf16[256,1792]{1,0:T(8,128)(2,1)S(1)}, u32[]{:S(2)}, u32[]{:S(2)}) collective-permute-start(bf16[256,1792]{1,0:T(8,128)(2,1)} %collective-permute-done.1.last), channel_id=1, source_target_pairs={{0,16},{16,0},{32,48},{48,32},{64,80},{80,64},{96,112},{112,96},{1... | collective-permute-start | bytes 2752520 | tf_op jit(solution)/shard_map/ppermute | solution.py:18
  64.3 28.8 %collective-permute-start.3 = (bf16[1792,256]{1,0:T(8,128)(2,1)S(1)}, bf16[1792,256]{1,0:T(8,128)(2,1)S(1)}, u32[]{:S(2)}, u32[]{:S(2)}) collective-permute-start(bf16[1792,256]{1,0:T(8,128)(2,1)S(1)} %copy-done), channel_id=1, source_target_pairs={{0,192},{16,208},{32,224},{48,240},{64,0},{80,16},{96,32},{112,48}... | collective-permute-start | bytes 2752520 | tf_op jit(solution)/shard_map/ppermute | solution.py:18
  96.6 13.6 %copy-start.4 = (s32[256]{0:T(256)S(1)}, s32[256]{0:T(256)}, u32[]{:S(2)}) copy-start(s32[256]{0:T(256)} %param.9) | copy-start | bytes 3076
  96.6 40.6 %all-to-all-start = ((s16[16,16,2176]{2,1,0:T(8,128)(2,1)}), s16[16,16,2176]{2,1,0:T(8,128)(2,1)S(1)}, u32[]{:S(2)}, u32[]{:S(2)}) async-start(s16[16,16,2176]{2,1,0:T(8,128)(2,1)} %bitcast.1), calls=%async_computation | async-start | bytes 2228224 | tf_op jit(solution)/shard_map/all_to_all | solution.py:147
  153.9 5.2 %collective-permute-start.10 = (f32[8,16]{1,0:T(8,128)S(1)}, f32[8,16]{1,0:T(8,128)S(1)}, u32[]{:S(2)}, u32[]{:S(2)}) collective-permute-start(f32[8,16]{1,0:T(8,128)S(1)} %slice.18), channel_id=1, source_target_pairs={{0,64},{16,80},{32,96},{48,112},{64,128},{80,144},{96,160},{112,17... | collective-permute-start | bytes 1544 | tf_op jit(solution)/shard_map/ppermute | solution.py:18
where the time goes:
time: 160 us
  waiting for transfers between devices  95.8 us (60%)
  starting transfers between devices  34.2 us (21%)
  blocking collectives  13.4 us (8%)
  Pallas kernels  11.1 us (7%)
  local copies, waits for them, and re-layouts  3.02 us (2%)
  other arithmetic  1.83 us (1%)
    ppermute x11, waiting for transfers between devices, moved(): return lax.ppermute(value, 'pb', pairs)  69.9 us
    all_to_all x2, waiting for transfers between devices, exchanged(): return lax.all_to_all(coded, 'wa', 0, 0, tiled=True)  25.9 us
    all_to_all x2, starting transfers between devices, exchanged(): return lax.all_to_all(coded, 'wa', 0, 0, tiled=True)  22.3 us
    all_to_all x1, blocking collectives, scores(): came = jnp.sum(lax.all_to_all(both, 'wa', 0, 0, tiled=True), axis=0)  13.4 us
    ppermute x11, starting transfers between devices, moved(): return lax.ppermute(value, 'pb', pairs)  11.9 us
    pallas_call x3, Pallas kernels, call(): pl.pallas_call(kernel, out_shape=jax.ShapeDtypeStruct((rows, lanes + LANE...  9.03 us
  transfers between devices with their start and end apart: 13, of which 6 were waited for; matrix products, arithmetic and copies ran while one was open for 0% of the time, Pallas kernels for 6%

commit v1 on v0

--- a/solution.py
+++ b/solution.py
@@ -208,10 +208,10 @@
         [came_in, outs, near_table, far_table],
     )
     share = nseq // widths
-    both = jnp.moveaxis(both.reshape(both.shape[0], widths, share), 1, 0)
-    came = jnp.sum(lax.all_to_all(both, "wa", 0, 0, tiled=True), axis=0)
     forward = [(p, (p + quarter) % groups) for p in range(groups)]
-    mine = came[:queries] + moved(came[queries:], forward)
+    total = both[:queries] + moved(both[queries:], forward)
+    total = jnp.moveaxis(total.reshape(queries, widths, share), 1, 0)
+    mine = jnp.sum(lax.all_to_all(total, "wa", 0, 0, tiled=True), axis=0)
     lengths_float = lengths.astype(jnp.float32)
     my_lengths = lax.dynamic_slice_in_dim(lengths_float, width_slot * share, share, 0)
     return mine / my_lengths[None, :]

time: 160 us -> 161 us (level)
  blocking collectives: 13.4 us -> 0 us
  waiting for transfers between devices: 95.8 us -> 104 us
  starting transfers between devices: 34.2 us -> 39.4 us
    all_to_all x1 -> x0, blocking collectives: 13.4 us -> none  [scores(): came = jnp.sum(lax.all_to_all(both, 'wa', 0, 0, tiled=True), axis=0)]
    all_to_all x0 -> x1, waiting for transfers between devices: none -> 8.4 us  [scores(): mine = jnp.sum(lax.all_to_all(total, 'wa', 0, 0, tiled=True), axis=0)]
    all_to_all x0 -> x1, starting transfers between devices: none -> 5.16 us  [scores(): mine = jnp.sum(lax.all_to_all(total, 'wa', 0, 0, tiled=True), axis=0)]
  transfers between devices with their start and end apart: 13 -> 14, of which waited for: 6 -> 7; matrix products, arithmetic and copies ran while one was open for 0% -> 0% of each run, Pallas kernels for 6% -> 6%
where the time goes in v1:
time: 161 us; the launch traced here: 160 us
  waiting for transfers between devices  104 us (65%)
  starting transfers between devices  39.4 us (24%)
  Pallas kernels  11 us (7%)
  local copies, waits for them, and re-layouts  3.55 us (2%)
  other arithmetic  1.82 us (1%)
    ppermute x11, waiting for transfers between devices, moved(): return lax.ppermute(value, 'pb', pairs)  70.1 us
    all_to_all x2, waiting for transfers between devices, exchanged(): return lax.all_to_all(coded, 'wa', 0, 0, tiled=True)  25.9 us
    all_to_all x2, starting transfers between devices, exchanged(): return lax.all_to_all(coded, 'wa', 0, 0, tiled=True)  22.3 us
    ppermute x11, starting transfers between devices, moved(): return lax.ppermute(value, 'pb', pairs)  11.9 us
    pallas_call x3, Pallas kernels, call(): pl.pallas_call(kernel, out_shape=jax.ShapeDtypeStruct((rows, lanes + LANE...  9.01 us
    all_to_all x1, waiting for transfers between devices, scores(): mine = jnp.sum(lax.all_to_all(total, 'wa', 0, 0, tiled=True), axis=0)  8.4 us
    all_to_all x1, starting transfers between devices, scores(): mine = jnp.sum(lax.all_to_all(total, 'wa', 0, 0, tiled=True), axis=0)  5.16 us
  transfers between devices with their start and end apart: 14, of which 7 were waited for; matrix products, arithmetic and copies ran while one was open for 0% of the time, Pallas kernels for 6%

profile of v1, /device:TPU:6, one launch (start us, length us, event | category | flops | bytes accessed | tf_op | source)
XLA Modules:
  0.0 160.5 jit_solution(14075181249335436426)
XLA Ops:
  0.0 3.1 %collective-permute-start.7 = (bf16[256,512]{1,0:T(8,128)(2,1)}, bf16[256,512]{1,0:T(8,128)(2,1)S(1)}, u32[]{:S(2)}, u32[]{:S(2)}) collective-permute-start(bf16[256,512]{1,0:T(8,128)(2,1)} %own.5), channel_id=1, source_target_pairs={{0,32},{16,48},{32,64},{48,80},{64,96},{80,112},{96,128},{112,144}... | collective-permute-start | bytes 786440 | tf_op jit(solution)/shard_map/ppermute | solution.py:18
  3.1 1.3 collective-permute-start.6
  4.4 0.1 collective-permute-start.9
  4.5 10.1 %collective-permute-done.7.last = bf16[256,512]{1,0:T(8,128)(2,1)S(1)} collective-permute-done((bf16[256,512]{1,0:T(8,128)(2,1)}, bf16[256,512]{1,0:T(8,128)(2,1)S(1)}, u32[]{:S(2)}, u32[]{:S(2)}) %collective-permute-start.7) | collective-permute-done | bytes 262176 | tf_op jit(solution)/shard_map/ppermute | solution.py:18
  14.6 6.0 %collective-permute-start.1 = (bf16[256,1792]{1,0:T(8,128)(2,1)}, bf16[256,1792]{1,0:T(8,128)(2,1)}, u32[]{:S(2)}, u32[]{:S(2)}) collective-permute-start(bf16[256,1792]{1,0:T(8,128)(2,1)} %own.4), channel_id=1, source_target_pairs={{0,32},{16,48},{32,64},{48,80},{64,96},{80,112},{96,128},{112,144}... | collective-permute-start | bytes 2752520 | tf_op jit(solution)/shard_map/ppermute | solution.py:18
  20.6 0.9 copy-done.2
  21.6 0.9 copy-done.3
  22.5 2.5 %shard_map.57 = s16[256,2176]{1,0:T(8,128)(2,1)} custom-call(s32[1]{0:T(128)} %bitcast.even, bf16[256,512]{1,0:T(8,128)(2,1)S(1)} %copy-done.2, bf16[256,512]{1,0:T(8,128)(2,1)S(1)} %collective-permute-done.5.side, bf16[256,512]{1,0:T(8,128)(2,1)S(1)} %collective-permute-done.6.flip, bf16[256,512]{1,0:T(8,128)(2,1)S(1)} %collective-permute-done.7.last, ...), custom_call_target="tpu_custom_call" | custom-call | flops 536870912 | bytes 2883584 | tf_op jit(solution)/shard_map/pallas_call | solution.py:131
  25.0 8.8 %all-to-all-start.1 = ((s16[16,16,2176]{2,1,0:T(8,128)(2,1)}), s16[16,16,2176]{2,1,0:T(8,128)(2,1)S(1)}, u32[]{:S(2)}, u32[]{:S(2)}) async-start(s16[16,16,2176]{2,1,0:T(8,128)(2,1)} %bitcast.3), calls=%async_computation.1 | async-start | bytes 2228224 | tf_op jit(solution)/shard_map/all_to_all | solution.py:147
  33.9 0.1 collective-permute-start
  34.0 1.3 collective-permute-start.4
  35.3 29.1 %collective-permute-done.1.last = bf16[256,1792]{1,0:T(8,128)(2,1)} collective-permute-done((bf16[256,1792]{1,0:T(8,128)(2,1)}, bf16[256,1792]{1,0:T(8,128)(2,1)}, u32[]{:S(2)}, u32[]{:S(2)}) %collective-permute-start.1) | collective-permute-done | bytes 917536 | tf_op jit(solution)/shard_map/ppermute | solution.py:18
  64.4 2.7 %collective-permute-done.2.lasts = bf16[256,1792]{1,0:T(8,128)(2,1)S(1)} collective-permute-done((bf16[256,1792]{1,0:T(8,128)(2,1)}, bf16[256,1792]{1,0:T(8,128)(2,1)S(1)}, u32[]{:S(2)}, u32[]{:S(2)}) %collective-permute-start.2) | collective-permute-done | bytes 917536 | tf_op jit(solution)/shard_map/ppermute | solution.py:18
  67.0 3.0 %shard_map.55.begun = s16[256,1152]{1,0:T(8,128)(2,1)S(1)} custom-call(s32[1]{0:T(128)} %bitcast.even, bf16[256,1792]{1,0:T(8,128)(2,1)S(1)} %copy-done.1, bf16[256,1792]{1,0:T(8,128)(2,1)S(1)} %collective-permute-done.side, bf16[256,1792]{1,0:T(8,128)(2,1)S(1)} %collective-permute-done.4.flip, bf16[256,1792]{1,0:T(8,128)(2,1)} %collective-permute-done.1.last, ...), custom_call_target="tpu_custom_call" | custom-call | flops 939524096 | bytes 6029312 | tf_op jit(solution)/shard_map/pallas_call | solution.py:131
  70.0 23.1 %collective-permute-done.3.far = bf16[1792,256]{1,0:T(8,128)(2,1)S(1)} collective-permute-done((bf16[1792,256]{1,0:T(8,128)(2,1)S(1)}, bf16[1792,256]{1,0:T(8,128)(2,1)S(1)}, u32[]{:S(2)}, u32[]{:S(2)}) %collective-permute-start.3) | collective-permute-done | bytes 917536 | tf_op jit(solution)/shard_map/ppermute | solution.py:18
  93.1 3.5 %shard_map.56 = s16[256,2176]{1,0:T(8,128)(2,1)} custom-call(s32[1]{0:T(128)} %bitcast.even, bf16[256,1792]{1,0:T(8,128)(2,1)S(1)} %copy-done.1, bf16[256,1792]{1,0:T(8,128)(2,1)S(1)} %collective-permute-done.side, bf16[256,1792]{1,0:T(8,128)(2,1)} %collective-permute-done.1.last, bf16[256,1792]{1,0:T(8,128)(2,1)S(1)} %collective-permute-done.2.lasts, ...), custom_call_target="tpu_custom_call" | custom-call | flops 1879048192 | bytes 6225920 | tf_op jit(solution)/shard_map/pallas_call | solution.py:131
  96.6 13.5 %all-to-all-start = ((s16[16,16,2176]{2,1,0:T(8,128)(2,1)}), s16[16,16,2176]{2,1,0:T(8,128)(2,1)S(1)}, u32[]{:S(2)}, u32[]{:S(2)}) async-start(s16[16,16,2176]{2,1,0:T(8,128)(2,1)} %bitcast.1), calls=%async_computation | async-start | bytes 2228224 | tf_op jit(solution)/shard_map/all_to_all | solution.py:147
  110.2 0.3 reduce-window.9
  110.6 0.1 slice_reduce_fusion
  110.8 0.1 and_convert_fusion
  110.9 0.4 shard_map.58.outs_ref
  111.3 25.9 %all-to-all-done = s16[16,16,2176]{2,1,0:T(8,128)(2,1)S(1)} async-done(((s16[16,16,2176]{2,1,0:T(8,128)(2,1)}), s16[16,16,2176]{2,1,0:T(8,128)(2,1)S(1)}, u32[]{:S(2)}, u32[]{:S(2)}) %all-to-all-start) | async-done | bytes 1114144 | tf_op jit(solution)/shard_map/all_to_all | solution.py:147
  137.2 1.7 %shard_map.59 = f32[16,256]{1,0:T(8,128)S(1)} custom-call(s16[256,2176]{1,0:T(8,128)(2,1)S(1)} %bitcast.13, f32[128,256]{1,0:T(8,128)S(1)} %shard_map.58.outs_ref, f32[64,256]{1,0:T(8,128)S(1)} %get-tuple-element.8.near_ref, f32[64,256]{1,0:T(8,128)S(1)} %get-tuple-element.7.far_ref), custom_call_target="tpu_custom_call" | custom-call | flops 2228224 | bytes 1114112 | tf_op jit(solution)/shard_map/pallas_call | solution.py:117
  138.9 0.1 collective-permute-start.10
  139.0 5.1 %collective-permute-done.10 = f32[8,256]{1,0:T(8,128)S(1)} collective-permute-done((f32[8,256]{1,0:T(8,128)S(1)}, f32[8,256]{1,0:T(8,128)S(1)}, u32[]{:S(2)}, u32[]{:S(2)}) %collective-permute-start.10) | collective-permute-done | bytes 8224 | tf_op jit(solution)/shard_map/ppermute | solution.py:18
  144.2 0.7 reshape.68
  144.9 5.2 %all-to-all-start.2 = ((f32[16,1,128]{2,1,0:T(1,128)}), f32[16,1,128]{2,1,0:T(1,128)S(1)}, u32[]{:S(2)}, u32[]{:S(2)}) async-start(f32[16,1,128]{2,1,0:T(1,128)} %reshape.68), calls=%async_computation.2 | async-start | bytes 16384 | tf_op jit(solution)/shard_map/all_to_all | solution.py:214
  150.1 0.1 dynamic_slice.3
  150.2 8.4 %all-to-all-done.2 = f32[16,1,128]{2,1,0:T(1,128)S(1)} async-done(((f32[16,1,128]{2,1,0:T(1,128)}), f32[16,1,128]{2,1,0:T(1,128)S(1)}, u32[]{:S(2)}, u32[]{:S(2)}) %all-to-all-start.2) | async-done | bytes 8224 | tf_op jit(solution)/shard_map/all_to_all | solution.py:214
  158.6 0.5 broadcast.36
  159.1 0.7 reduce.2
  159.9 0.6 broadcast_divide_fusion
  (32 shorter events, 0.5 us)
Async XLA Ops:
  0.0 14.6 %collective-permute-start.7 = (bf16[256,512]{1,0:T(8,128)(2,1)}, bf16[256,512]{1,0:T(8,128)(2,1)S(1)}, u32[]{:S(2)}, u32[]{:S(2)}) collective-permute-start(bf16[256,512]{1,0:T(8,128)(2,1)} %own.5), channel_id=1, source_target_pairs={{0,32},{16,48},{32,64},{48,80},{64,96},{80,112},{96,128},{112,144}... | collective-permute-start | bytes 786440 | tf_op jit(solution)/shard_map/ppermute | solution.py:18
  3.1 17.5 %collective-permute-start.5 = (bf16[256,512]{1,0:T(8,128)(2,1)}, bf16[256,512]{1,0:T(8,128)(2,1)S(1)}, u32[]{:S(2)}, u32[]{:S(2)}) collective-permute-start(bf16[256,512]{1,0:T(8,128)(2,1)} %own.5), channel_id=1, source_target_pairs={{0,16},{16,0},{32,48},{48,32},{64,80},{80,64},{96,112},{112,96},{1... | collective-permute-start | bytes 786440 | tf_op jit(solution)/shard_map/ppermute | solution.py:18
  3.1 17.5 %collective-permute-start.6 = (bf16[256,512]{1,0:T(8,128)(2,1)}, bf16[256,512]{1,0:T(8,128)(2,1)S(1)}, u32[]{:S(2)}, u32[]{:S(2)}) collective-permute-start(bf16[256,512]{1,0:T(8,128)(2,1)} %own.5), channel_id=1, source_target_pairs={{16,128},{48,160},{80,192},{112,224},{144,0},{176,32},{208,64},{24... | collective-permute-start | bytes 786440 | tf_op jit(solution)/shard_map/ppermute | solution.py:18
  4.4 16.2 %collective-permute-start.9 = (bf16[512,256]{1,0:T(8,128)(2,1)}, bf16[512,256]{1,0:T(8,128)(2,1)S(1)}, u32[]{:S(2)}, u32[]{:S(2)}) collective-permute-start(bf16[512,256]{1,0:T(8,128)(2,1)} %near.3), channel_id=1, source_target_pairs={{0,192},{16,208},{32,224},{48,240},{64,0},{80,16},{96,32},{112,48}... | collective-permute-start | bytes 786440 | tf_op jit(solution)/shard_map/ppermute | solution.py:18
  14.6 6.0 %collective-permute-start.8 = (bf16[256,512]{1,0:T(8,128)(2,1)S(1)}, bf16[256,512]{1,0:T(8,128)(2,1)S(1)}, u32[]{:S(2)}, u32[]{:S(2)}) collective-permute-start(bf16[256,512]{1,0:T(8,128)(2,1)S(1)} %collective-permute-done.7.last), channel_id=1, source_target_pairs={{0,16},{16,0},{32,48},{48,32},{64,80},{80,64},{96,112},{112,96},{1... | collective-permute-start | bytes 786440 | tf_op jit(solution)/shard_map/ppermute | solution.py:18
  14.6 49.7 %collective-permute-start.1 = (bf16[256,1792]{1,0:T(8,128)(2,1)}, bf16[256,1792]{1,0:T(8,128)(2,1)}, u32[]{:S(2)}, u32[]{:S(2)}) collective-permute-start(bf16[256,1792]{1,0:T(8,128)(2,1)} %own.4), channel_id=1, source_target_pairs={{0,32},{16,48},{32,64},{48,80},{64,96},{80,112},{96,128},{112,144}... | collective-permute-start | bytes 2752520 | tf_op jit(solution)/shard_map/ppermute | solution.py:18
  20.6 1.0 copy-start.2
  21.6 0.9 copy-start.3
  25.0 8.8 %copy-start.1 = (bf16[256,1792]{1,0:T(8,128)(2,1)S(1)}, bf16[256,1792]{1,0:T(8,128)(2,1)}, u32[]{:S(2)}) copy-start(bf16[256,1792]{1,0:T(8,128)(2,1)} %own.4) | copy-start | bytes 2752516
  25.0 39.3 %copy-start = (bf16[1792,256]{1,0:T(8,128)(2,1)S(1)}, bf16[1792,256]{1,0:T(8,128)(2,1)}, u32[]{:S(2)}) copy-start(bf16[1792,256]{1,0:T(8,128)(2,1)} %near.2) | copy-start | bytes 2752516
  25.0 71.6 %all-to-all-start.1 = ((s16[16,16,2176]{2,1,0:T(8,128)(2,1)}), s16[16,16,2176]{2,1,0:T(8,128)(2,1)S(1)}, u32[]{:S(2)}, u32[]{:S(2)}) async-start(s16[16,16,2176]{2,1,0:T(8,128)(2,1)} %bitcast.3), calls=%async_computation.1 | async-start | bytes 2228224 | tf_op jit(solution)/shard_map/all_to_all | solution.py:147
  33.9 30.5 %collective-permute-start = (bf16[256,1792]{1,0:T(8,128)(2,1)S(1)}, bf16[256,1792]{1,0:T(8,128)(2,1)S(1)}, u32[]{:S(2)}, u32[]{:S(2)}) collective-permute-start(bf16[256,1792]{1,0:T(8,128)(2,1)S(1)} %copy-done.1), channel_id=1, source_target_pairs={{0,16},{16,0},{32,48},{48,32},{64,80},{80,64},{96,112},{112,96},{1... | collective-permute-start | bytes 2752520 | tf_op jit(solution)/shard_map/ppermute | solution.py:18
  34.0 30.4 %collective-permute-start.4 = (bf16[256,1792]{1,0:T(8,128)(2,1)S(1)}, bf16[256,1792]{1,0:T(8,128)(2,1)S(1)}, u32[]{:S(2)}, u32[]{:S(2)}) collective-permute-start(bf16[256,1792]{1,0:T(8,128)(2,1)S(1)} %copy-done.1), channel_id=1, source_target_pairs={{16,128},{48,160},{80,192},{112,224},{144,0},{176,32},{208,64},{24... | collective-permute-start | bytes 2752520 | tf_op jit(solution)/shard_map/ppermute | solution.py:18
  64.3 2.7 %collective-permute-start.2 = (bf16[256,1792]{1,0:T(8,128)(2,1)}, bf16[256,1792]{1,0:T(8,128)(2,1)S(1)}, u32[]{:S(2)}, u32[]{:S(2)}) collective-permute-start(bf16[256,1792]{1,0:T(8,128)(2,1)} %collective-permute-done.1.last), channel_id=1, source_target_pairs={{0,16},{16,0},{32,48},{48,32},{64,80},{80,64},{96,112},{112,96},{1... | collective-permute-start | bytes 2752520 | tf_op jit(solution)/shard_map/ppermute | solution.py:18
  64.3 28.8 %collective-permute-start.3 = (bf16[1792,256]{1,0:T(8,128)(2,1)S(1)}, bf16[1792,256]{1,0:T(8,128)(2,1)S(1)}, u32[]{:S(2)}, u32[]{:S(2)}) collective-permute-start(bf16[1792,256]{1,0:T(8,128)(2,1)S(1)} %copy-done), channel_id=1, source_target_pairs={{0,192},{16,208},{32,224},{48,240},{64,0},{80,16},{96,32},{112,48}... | collective-permute-start | bytes 2752520 | tf_op jit(solution)/shard_map/ppermute | solution.py:18
  96.6 13.5 %copy-start.4 = (s32[256]{0:T(256)S(1)}, s32[256]{0:T(256)}, u32[]{:S(2)}) copy-start(s32[256]{0:T(256)} %param.9) | copy-start | bytes 3076
  96.6 40.6 %all-to-all-start = ((s16[16,16,2176]{2,1,0:T(8,128)(2,1)}), s16[16,16,2176]{2,1,0:T(8,128)(2,1)S(1)}, u32[]{:S(2)}, u32[]{:S(2)}) async-start(s16[16,16,2176]{2,1,0:T(8,128)(2,1)} %bitcast.1), calls=%async_computation | async-start | bytes 2228224 | tf_op jit(solution)/shard_map/all_to_all | solution.py:147
  138.9 5.2 %collective-permute-start.10 = (f32[8,256]{1,0:T(8,128)S(1)}, f32[8,256]{1,0:T(8,128)S(1)}, u32[]{:S(2)}, u32[]{:S(2)}) collective-permute-start(f32[8,256]{1,0:T(8,128)S(1)} %slice.18), channel_id=1, source_target_pairs={{0,64},{16,80},{32,96},{48,112},{64,128},{80,144},{96,160},{112,17... | collective-permute-start | bytes 24584 | tf_op jit(solution)/shard_map/ppermute | solution.py:18
  144.9 13.7 %all-to-all-start.2 = ((f32[16,1,128]{2,1,0:T(1,128)}), f32[16,1,128]{2,1,0:T(1,128)S(1)}, u32[]{:S(2)}, u32[]{:S(2)}) async-start(f32[16,1,128]{2,1,0:T(1,128)} %reshape.68), calls=%async_computation.2 | async-start | bytes 16384 | tf_op jit(solution)/shard_map/all_to_all | solution.py:214
